TPU v7x, 128 devices: a whole 4x4x4 slice. The times are simulated.
128 devices in a mesh: row: 8 (over x_hi, z), col: 16 (over x_lo, y, core).
Axes of the slice: x: 4 (x_hi: 2, x_lo: 2; x = x_hi * 2 + x_lo), y: 4, z: 4, core: 2. Of those that a mesh axis runs over, the one named last changes fastest.
Arguments:
- tokens: bfloat16 [1024, 12288], P('row', 'col'), may hold values from -6 to 6
- prev_tokens: bfloat16 [1024, 12288], P('row', 'col'), may hold values from -6 to 6
- hidden_grad: bfloat16 [1024, 49152], P('col', 'row'), may hold values from -6 to 6
- active_blocks: int32 [1], replicated, may hold values from 6 to 16
- weight: bfloat16 [12288, 49152], P('col', 'row'), may hold values from -0.0546875 to 0.0546875
Outputs:
- activation: bfloat16 [1024, 49152], P('col', 'row')
- weight_grad: bfloat16 [12288, 49152], P('col', 'row')
Inputs may be any that keep to these rules, and one draw needn't show every extreme that they name: The sampled blocks are the first active_blocks[0] blocks of 3072 hidden units.
All inputs are finite; a program needn't handle non-finite values.
Results may differ from a plain program's by a relative error of at most 0.001.
Values may be sent and summed in bfloat16 or wider, within the bound.
A program may use at most 640 MiB of HBM per device.

v0:
```python
import jax
import jax.numpy as jnp
from jax import lax
from jax.sharding import PartitionSpec as P

BLOCK = 3072


def in_one_piece(arrays, axis, dim, along):
    both = jnp.concatenate(arrays, axis=along)
    result, at, outs = (lax.all_gather(both, axis, axis=dim, tiled=True), 0, [])
    for a in arrays:
        outs.append(lax.slice_in_dim(result, at, at + a.shape[along], axis=along))
        at += a.shape[along]
    return tuple(outs)


def shards(tokens, prev_tokens, hidden_grad, active_blocks, weight):
    local_units = weight.shape[1]
    first_unit = lax.axis_index("row") * local_units
    unit_limit = active_blocks[0] * BLOCK
    unit_ids = first_unit + lax.iota(jnp.int32, local_units)
    unit_mask = (unit_ids < unit_limit).astype(jnp.float32)
    gathered, earlier = in_one_piece((tokens, prev_tokens), "row", 0, 1)
    hidden = lax.psum_scatter(
        jnp.dot(gathered, weight, preferred_element_type=jnp.float32),
        "col",
        scatter_dimension=0,
        tiled=True,
    )
    activation = (jax.nn.gelu(hidden, approximate=False) * unit_mask).astype(jnp.bfloat16)
    grad_sum = lax.dot_general(
        earlier,
        lax.all_gather(hidden_grad, "col", axis=0, tiled=True),
        (((0,), (0,)), ((), ())),
        preferred_element_type=jnp.float32,
    )
    weight_grad = (grad_sum * unit_mask).astype(jnp.bfloat16)
    return (activation, weight_grad)


def solution(mesh):
    return jax.shard_map(
        shards,
        mesh=mesh,
        in_specs=(P("row", "col"), P("row", "col"), P("col", "row"), P(), P("col", "row")),
        out_specs=(P("col", "row"), P("col", "row")),
        check_vma=False,
    )
```

profile of v0, /device:TPU:0, one launch (start us, length us, event | category | flops | bytes accessed | tf_op | source)
XLA Modules:
  0.0 303.0 jit_solution(265817429871638443)
XLA Ops:
  7.2 0.0 all-gather.3.cloned.1.call-start
  7.2 1.8 pad_maximum_fusion
  9.0 0.0 all-gather.3.cloned.1.call-update
  9.0 0.0 all-gather.5.cloned.1.call-start
  9.1 0.7 all-gather.5.cloned.1.call-update
  9.8 0.0 reduce-scatter.2.cloned.1.call-start
  9.8 66.0 %all-gather.3.cloned.1.call-done = bf16[1024,1536]{1,0:T(8,128)(2,1)} async-done(((bf16[128,1536]{1,0:T(8,128)(2,1)}), bf16[1024,1536]{1,0:T(8,128)(2,1)}) %all-gather.3.cloned.1.call-update) | async-done | bytes 3145744 | tf_op jit(solution)/shard_map/all_gather | solution.py:11
  75.8 17.5 %fusion.5 = f32[1024,6144]{1,0:T(8,128)} fusion(bf16[768,6144]{1,0:T(8,128)(2,1)} %param.9, bf16[1024,1536]{1,0:T(8,128)(2,1)} %all-gather.3.cloned.1.call-done), kind=kOutput, calls=%fused_computation.7 | convolution fusion | flops 9663676416 | bytes 36175872 | tf_op jit(solution)/shard_map/dot_general | solution.py:26
  93.3 0.0 copy-start
  93.3 0.0 reduce-scatter.2.cloned.1.call-update
  94.2 52.9 %all-gather.5.cloned.1.call-done = bf16[1024,6144]{1,0:T(8,128)(2,1)} async-done(((bf16[64,6144]{1,0:T(8,128)(2,1)}), bf16[1024,6144]{1,0:T(8,128)(2,1)}) %all-gather.5.cloned.1.call-update) | async-done | bytes 12582928 | tf_op jit(solution)/shard_map/all_gather | solution.py:34
  147.1 0.0 copy-done
  147.1 16.8 %multiply_convert_fusion = bf16[768,6144]{1,0:T(8,128)(2,1)} fusion(bf16[1024,6144]{1,0:T(8,128)(2,1)} %all-gather.5.cloned.1.call-done, f32[6144]{0:T(1024)S(1)} %fusion.14, bf16[1024,1536]{1,0:T(8,128)(2,1)S(1)} %copy-done), kind=kOutput, calls=%fused_computation | convolution fusion | flops 9673113600 | bytes 23617536 | tf_op jit(solution)/shard_map/dot_general | solution.py:32
  163.8 127.4 %reduce-scatter.2.cloned.1.call-done = f32[64,6144]{1,0:T(8,128)} async-done(((f32[1024,6144]{1,0:T(8,128)}), f32[64,6144]{1,0:T(8,128)}) %reduce-scatter.2.cloned.1.call-update) | async-done | bytes 1572880 | tf_op jit(solution)/shard_map/reduce_scatter | solution.py:25
  291.2 5.3 %fusion.3 = bf16[64,6144]{1,0:T(8,128)(2,1)} fusion(f32[64,6144]{1,0:T(8,128)} %reduce-scatter.2.cloned.1.call-done, f32[6144]{0:T(1024)S(1)} %fusion.14), kind=kLoop, calls=%fused_computation.5 | loop fusion | flops 25952256 | bytes 2383872 | tf_op jit(solution)/shard_map/convert_element_type | solution.py:31
  (1 shorter events, 0.0 us)
Async XLA Ops:
  7.2 68.6 %all-gather.3.cloned.1.call-start = ((), (), s32[]{:S(2)}) async-start(), calls=%async_computation.1 | async-start | bytes 3538944 | tf_op jit(solution)/shard_map/all_gather | solution.py:11
  9.0 138.0 %all-gather.5.cloned.1.call-start = ((), (), s32[]{:S(2)}) async-start(), calls=%async_computation.3 | async-start | bytes 13369344 | tf_op jit(solution)/shard_map/all_gather | solution.py:34
  9.8 281.4 %reduce-scatter.2.cloned.1.call-start = ((), (), s32[]{:S(2)}) async-start(), calls=%async_computation.2 | async-start | bytes 26738688 | tf_op jit(solution)/shard_map/reduce_scatter | solution.py:25
  93.3 53.7 %copy-start = (bf16[1024,1536]{1,0:T(8,128)(2,1)S(1)}, bf16[1024,1536]{1,0:T(8,128)(2,1)}, u32[]{:S(2)}) copy-start(bf16[1024,1536]{1,0:T(8,128)(2,1)} %all-gather.3.cloned.1.call-done) | copy-start | bytes 9437188
Sparse Core Ops, SparseCore 0:
  10.8 64.8 all-gather.2
  77.5 69.5 all-gather.4
  149.5 141.6 reduce-scatter.1
where the time goes:
time: 303 us
  waiting for transfers between devices  247 us (82%)
  matrix products  34.3 us (11%)
  between operations  14.6 us (5%)
  other arithmetic  7.08 us (2%)
    reduce_scatter x1, waiting for transfers between devices, shards(): lax.psum_scatter(jnp.dot(gathered, weight, preferred_element_type=jnp.flo...  127 us
    all_gather x1, waiting for transfers between devices, in_one_piece(): result, at, outs = (lax.all_gather(both, axis, axis=dim, tiled=True), 0, [])  66 us
    all_gather x1, waiting for transfers between devices, shards(): lax.all_gather(hidden_grad, 'col', axis=0, tiled=True)  52.9 us
    dot_general x1, matrix products, shards(): jnp.dot(gathered, weight, preferred_element_type=jnp.float32)  17.5 us
    dot_general x1, matrix products, shards(): lax.dot_general(earlier, lax.all_gather(hidden_grad, 'col', axis=0, tiled...  16.8 us
  transfers between devices with their start and end apart: 3, of which 3 were waited for; matrix products, arithmetic and copies ran while one was open for 11% of the time, Pallas kernels for 0%

commit v1 on v0

--- a/solution.py
+++ b/solution.py
@@ -4,6 +4,13 @@
 from jax.sharding import PartitionSpec as P
 
 BLOCK = 3072
+
+
+def exchange_gather(value, name, along):
+    size = lax.axis_size(name)
+    blocks = jnp.stack([value for _ in range(size)])
+    blocks = lax.all_to_all(blocks, name, split_axis=0, concat_axis=0)
+    return jnp.concatenate(blocks, axis=along)
 
 
 def in_one_piece(arrays, axis, dim, along):
@@ -31,7 +38,7 @@
     activation = (jax.nn.gelu(hidden, approximate=False) * unit_mask).astype(jnp.bfloat16)
     grad_sum = lax.dot_general(
         earlier,
-        lax.all_gather(hidden_grad, "col", axis=0, tiled=True),
+        exchange_gather(hidden_grad, "col", 0),
         (((0,), (0,)), ((), ())),
         preferred_element_type=jnp.float32,
     )

time: 303 us -> 401 us (1.32)
  waiting for transfers between devices: 247 us -> 331 us
  local copies, waits for them, and re-layouts: 0.01 us -> 7.98 us
  starting transfers between devices: 0.12 us -> 5.33 us
    all_to_all x0 -> x1, waiting for transfers between devices: none -> 220 us  [exchange_gather(): blocks = lax.all_to_all(blocks, name, split_axis=0, concat_axis=0)]
    reduce_scatter x1, waiting for transfers between devices: 127 us -> 44.6 us  [shards(): lax.psum_scatter(jnp.dot(gathered, weight, preferred_element_type=jnp.flo...]
    all_gather x1 -> x0, waiting for transfers between devices: 52.9 us -> none  [shards(): lax.all_gather(hidden_grad, 'col', axis=0, tiled=True)]
    another operation x0 -> x1, local copies, waits for them, and re-layouts: none -> 6.86 us  [exchange_gather(): blocks = jnp.stack([value for _ in range(size)])]
    all_to_all x0 -> x1, starting transfers between devices: none -> 5.25 us  [exchange_gather(): blocks = lax.all_to_all(blocks, name, split_axis=0, concat_axis=0)]
  transfers between devices with their start and end apart: 3 -> 3, of which waited for: 3 -> 3; matrix products, arithmetic and copies ran while one was open for 11% -> 6% of each run, Pallas kernels for 0% -> 0%
where the time goes in v1:
time: 401 us
  waiting for transfers between devices  331 us (83%)
  matrix products  34.5 us (9%)
  between operations  14.7 us (4%)
  local copies, waits for them, and re-layouts  7.98 us (2%)
  other arithmetic  7.08 us (2%)
  starting transfers between devices  5.33 us (1%)
    all_to_all x1, waiting for transfers between devices, exchange_gather(): blocks = lax.all_to_all(blocks, name, split_axis=0, concat_axis=0)  220 us
    all_gather x1, waiting for transfers between devices, in_one_piece(): result, at, outs = (lax.all_gather(both, axis, axis=dim, tiled=True), 0, [])  66.7 us
    reduce_scatter x1, waiting for transfers between devices, shards(): lax.psum_scatter(jnp.dot(gathered, weight, preferred_element_type=jnp.flo...  44.6 us
    dot_general x1, matrix products, shards(): jnp.dot(gathered, weight, preferred_element_type=jnp.float32)  17.5 us
    dot_general x1, matrix products, shards(): lax.dot_general(earlier, exchange_gather(hidden_grad, 'col', 0), (((0,),...  16.9 us
  transfers between devices with their start and end apart: 3, of which 3 were waited for; matrix products, arithmetic and copies ran while one was open for 6% of the time, Pallas kernels for 0%

profile of v1, /device:TPU:0, one launch (start us, length us, event | category | flops | bytes accessed | tf_op | source)
XLA Modules:
  0.0 401.0 jit_solution(17682584979167287456)
XLA Ops:
  7.2 0.0 all-gather.2.cloned.1.call-start
  7.2 1.8 pad_maximum_fusion
  9.0 0.0 all-gather.2.cloned.1.call-update
  9.0 0.0 reduce-scatter.2.cloned.1.call-start
  9.1 66.7 %all-gather.2.cloned.1.call-done = bf16[1024,1536]{1,0:T(8,128)(2,1)} async-done(((bf16[128,1536]{1,0:T(8,128)(2,1)}), bf16[1024,1536]{1,0:T(8,128)(2,1)}) %all-gather.2.cloned.1.call-update) | async-done | bytes 3145744 | tf_op jit(solution)/shard_map/all_gather | solution.py:18
  75.8 17.5 %fusion.5 = f32[1024,6144]{1,0:T(8,128)} fusion(bf16[768,6144]{1,0:T(8,128)(2,1)} %param.9, bf16[1024,1536]{1,0:T(8,128)(2,1)} %all-gather.2.cloned.1.call-done), kind=kOutput, calls=%fused_computation.7 | convolution fusion | flops 9663676416 | bytes 36175872 | tf_op jit(solution)/shard_map/dot_general | solution.py:33
  93.3 0.0 copy-start
  93.3 0.0 reduce-scatter.2.cloned.1.call-update
  93.4 1.1 copy-done
  94.5 6.9 %stack.2 = bf16[16,64,6144]{2,1,0:T(8,128)(2,1)} broadcast(bf16[64,6144]{1,0:T(8,128)(2,1)S(1)} %copy-done), dimensions={1,2} | broadcast | bytes 13369344 | tf_op jit(solution)/shard_map/stack | solution.py:11
  101.3 0.0 copy-start.1
  101.3 5.3 %all-to-all-start = ((bf16[16,64,6144]{2,1,0:T(8,128)(2,1)}), bf16[16,64,6144]{2,1,0:T(8,128)(2,1)}, u32[]{:S(2)}, u32[]{:S(2)}) async-start(bf16[16,64,6144]{2,1,0:T(8,128)(2,1)} %stack.2), calls=%async_computation.1 | async-start | bytes 25165824 | tf_op jit(solution)/shard_map/all_to_all | solution.py:12
  107.3 220.2 %all-to-all-done = bf16[16,64,6144]{2,1,0:T(8,128)(2,1)} async-done(((bf16[16,64,6144]{2,1,0:T(8,128)(2,1)}), bf16[16,64,6144]{2,1,0:T(8,128)(2,1)}, u32[]{:S(2)}, u32[]{:S(2)}) %all-to-all-start) | async-done | bytes 12582944 | tf_op jit(solution)/shard_map/all_to_all | solution.py:12
  327.4 0.0 copy-done.1
  327.4 16.9 %multiply_convert_fusion = bf16[768,6144]{1,0:T(8,128)(2,1)} fusion(bf16[1024,6144]{1,0:T(8,128)(2,1)} %bitcast.1, f32[6144]{0:T(1024)S(1)} %fusion.14, bf16[1024,1536]{1,0:T(8,128)(2,1)S(1)} %copy-done.1), kind=kOutput, calls=%fused_computation | convolution fusion | flops 9673113600 | bytes 23617536 | tf_op jit(solution)/shard_map/dot_general | solution.py:39
  344.3 44.6 %reduce-scatter.2.cloned.1.call-done = f32[64,6144]{1,0:T(8,128)} async-done(((f32[1024,6144]{1,0:T(8,128)}), f32[64,6144]{1,0:T(8,128)}) %reduce-scatter.2.cloned.1.call-update) | async-done | bytes 1572880 | tf_op jit(solution)/shard_map/reduce_scatter | solution.py:32
  388.9 5.3 %fusion.3 = bf16[64,6144]{1,0:T(8,128)(2,1)} fusion(f32[64,6144]{1,0:T(8,128)} %reduce-scatter.2.cloned.1.call-done, f32[6144]{0:T(1024)S(1)} %fusion.14), kind=kLoop, calls=%fused_computation.5 | loop fusion | flops 25952256 | bytes 2383872 | tf_op jit(solution)/shard_map/convert_element_type | solution.py:38
  (1 shorter events, 0.0 us)
Async XLA Ops:
  7.2 68.6 %all-gather.2.cloned.1.call-start = ((), (), s32[]{:S(2)}) async-start(), calls=%async_computation.2 | async-start | bytes 3538944 | tf_op jit(solution)/shard_map/all_gather | solution.py:18
  9.0 379.9 %reduce-scatter.2.cloned.1.call-start = ((), (), s32[]{:S(2)}) async-start(), calls=%async_computation.3 | async-start | bytes 26738688 | tf_op jit(solution)/shard_map/reduce_scatter | solution.py:32
  93.3 1.1 copy-start
  101.3 226.1 %copy-start.1 = (bf16[1024,1536]{1,0:T(8,128)(2,1)S(1)}, bf16[1024,1536]{1,0:T(8,128)(2,1)}, u32[]{:S(2)}) copy-start(bf16[1024,1536]{1,0:T(8,128)(2,1)} %all-gather.2.cloned.1.call-done) | copy-start | bytes 9437188
  101.3 226.1 %all-to-all-start = ((bf16[16,64,6144]{2,1,0:T(8,128)(2,1)}), bf16[16,64,6144]{2,1,0:T(8,128)(2,1)}, u32[]{:S(2)}, u32[]{:S(2)}) async-start(bf16[16,64,6144]{2,1,0:T(8,128)(2,1)} %stack.2), calls=%async_computation.1 | async-start | bytes 25165824 | tf_op jit(solution)/shard_map/all_to_all | solution.py:12
Sparse Core Ops, SparseCore 0:
  10.8 64.8 all-gather.1
  93.5 295.4 reduce-scatter.1
